TPU v7x, 32 devices: a whole 2x2x4 slice. The times are simulated.
32 devices in a mesh: rows: 32 (over z, y, x, core).
Axes of the slice: x: 2, y: 2, z: 4, core: 2. Of those that a mesh axis runs over, the one named last changes fastest.
Arguments:
- source: float32 [64, 131072], P(None, 'rows'), may hold values from -6 to 6
- band_values: float32 [128, 131072], P(None, 'rows'), may hold values from -0.625 to 0.625
- offsets: int32 [128], replicated, may hold values from -128 to 128, as said below
Outputs:
- compressed: float32 [128, 131072], P(None, 'rows')
Inputs may be any that keep to these rules, and one draw needn't show every extreme that they name: The 128 offsets are distinct and include both -128 and 128.
All inputs are finite; a program needn't handle non-finite values.
Results may differ from a plain program's by a relative error of at most 0.0003.
Values sent between devices are 32-bit elements; how exact they have to be, the bound alone decides.
A program may use at most 192 MiB of HBM per device.

v0:
```python
import jax
import jax.numpy as jnp
from jax import lax
from jax.sharding import PartitionSpec as P

HB = 128
K2 = 128


def padded(block, sides, width):
    for axis, dim in sides:
        count = lax.axis_size(axis)
        forward = [(i, i + 1) for i in range(count - 1)]
        backward = [(target, source) for source, target in forward]
        low = lax.ppermute(
            lax.slice_in_dim(block, block.shape[dim] - width, None, axis=dim), axis, forward
        )
        high = lax.ppermute(lax.slice_in_dim(block, 0, width, axis=dim), axis, backward)
        block = jnp.concatenate([low, block, high], axis=dim)
    return block


def band_blocks(band_values, offsets):
    diagonals = band_values.shape[0]
    blocks = band_values.shape[1] // HB
    values = band_values.reshape(diagonals, blocks, HB).transpose(1, 0, 2)
    within = jnp.arange(HB, dtype=jnp.int32)
    columns = within[None, :] + offsets[:, None] + HB
    row_index = jnp.broadcast_to(within[None, :], columns.shape)
    blocked = jnp.zeros((blocks, HB, 3 * HB), values.dtype)
    return blocked.at[:, row_index, columns].set(values)


def apply_band(extended, blocked):
    width = extended.shape[0]
    blocks = blocked.shape[0]
    pieces = extended.reshape(width, blocks + 2, HB)
    windows = jnp.concatenate([pieces[:, :-2], pieces[:, 1:-1], pieces[:, 2:]], axis=2)
    result = jnp.einsum("cbj,brj->cbr", windows, blocked, precision=lax.Precision.HIGHEST)
    return result.reshape(width, blocks * HB)


def compress(grammian, retain):
    spanning = grammian[:, :retain]
    coeffs = None
    for repeat in range(2):
        if repeat > 0:
            spanning = jnp.dot(grammian, coeffs.T, precision=lax.Precision.HIGHEST)
        mapped = jnp.dot(grammian, spanning, precision=lax.Precision.HIGHEST)
        metric = jnp.dot(spanning.T, mapped, precision=lax.Precision.HIGHEST)
        metric = 0.5 * (metric + metric.T)
        factor = jnp.linalg.cholesky(metric)
        coeffs = jax.scipy.linalg.solve_triangular(factor, spanning.T, lower=True)
    return coeffs


def gram_total(stacked, total):
    local = jnp.dot(stacked, stacked.T, precision=lax.Precision.HIGHEST)
    summed = lax.psum(local, "rows")
    return summed / total


def first_gram(first, total):
    return gram_total(first, total)


def second_gram(factor, squared, total):
    return gram_total(jnp.concatenate([factor, squared], axis=0), total)


def body(source, band_values, offsets):
    devices_here = lax.axis_size("rows")
    total = float(source.shape[1] * devices_here)
    keep_first = 2 * source.shape[0]
    deep_source = padded(source, (("rows", 1),), 3 * HB)
    deep_band = padded(band_values, (("rows", 1),), 2 * HB)
    blocked = band_blocks(deep_band, offsets)
    first_deep = jnp.concatenate([deep_source[:, HB:-HB], apply_band(deep_source, blocked)], axis=0)
    first = first_deep[:, 2 * HB : -2 * HB]
    gram_one = first_gram(first, total)
    coeffs_one = compress(gram_one, keep_first)
    factor_deep = jnp.dot(coeffs_one, first_deep, precision=lax.Precision.HIGHEST)
    factor = factor_deep[:, 2 * HB : -2 * HB]
    once_more = apply_band(factor_deep, blocked[1:-1])
    squared = apply_band(once_more, blocked[2:-2])
    second = jnp.concatenate([factor, squared], axis=0)
    coeffs_two = compress(second_gram(factor, squared, total), K2)
    return jnp.dot(coeffs_two, second, precision=lax.Precision.HIGHEST)


def solution(mesh):
    placed = (P(None, "rows"), P(None, "rows"), P())
    return jax.shard_map(
        body, mesh=mesh, in_specs=placed, out_specs=P(None, "rows"), check_vma=False
    )
```

profile of v0, /device:TPU:0, one launch (start us, length us, event | category | flops | bytes accessed | tf_op | source)
XLA Modules:
  0.0 541.9 jit_solution(10150455950687637669)
XLA Ops:
  6.6 2.0 copy.71
  8.6 0.7 fusion.101
  9.3 1.3 collective-permute-start.3
  10.6 3.7 collective-permute-start.2
  14.3 3.9 collective-permute-start
  18.2 1.3 collective-permute-start.1
  19.8 0.6 select_bitcast_fusion
  20.4 0.6 constant_dynamic-update-slice_fusion.2
  21.1 1.0 constant_dynamic-update-slice_fusion.1
  22.1 0.6 constant_dynamic-update-slice_fusion
  22.8 1.5 reshape.80
  24.5 1.4 slice.90
  25.9 1.2 copy.105
  27.1 1.2 copy.104
  28.3 1.2 copy.103
  29.6 2.5 pad_maximum_fusion.3
  32.0 8.6 %copy.98 = f32[128,128,36]{2,1,0:T(8,128)} copy(f32[128,128,36]{0,1,2:T(8,128)} %bitcast.109) | data formatting | bytes 4718592 | tf_op jit(solution)/shard_map/transpose | solution.py:26
  40.6 51.0 %scatter_custom_fusion = f32[36,49152]{0,1:T(8,128)} fusion(s32[16384]{0:T(1024)} %select_bitcast_fusion, f32[16384,36]{1,0:T(8,128)} %bitcast.111, f32[]{:T(128)} %constant.47.clone.1), kind=kCustom, calls=%fused_computation.1 | custom fusion | bytes 7078400
  91.7 17.8 %copy.79 = f32[36,128,384]{2,1,0:T(8,128)} copy(f32[36,128,384]{0,2,1:T(8,128)} %bitcast.101) | data formatting | bytes 14155776 | tf_op jit(solution)/shard_map/scatter | solution.py:31
  109.5 12.0 %fusion.33 = f32[36,8,8,128]{3,2,1,0:T(8,128)S(1)} fusion(f32[36,128,384]{2,1,0:T(8,128)} %copy.79, f32[64,36,128]{2,0,1:T(8,128)S(1)} %copy-done.2, f32[64,36,128]{2,0,1:T(8,128)S(1)} %copy-done.3, f32[64,36,128]{2,0,1:T(8,128)} %copy.103), kind=kOutput, calls=%fused_computation.34 | convolution fusion | flops 1360723968 | bytes 11796480 | tf_op jit(solution)/shard_map/cbj,brj->cbr/dot_general | solution.py:39
  121.5 2.4 fusion.26
  124.0 18.9 %slice.97 = f32[32,49152]{0,1:T(8,128)} slice(f32[36,49152]{0,1:T(8,128)} %scatter_custom_fusion), slice={[2:34], [0:49152]} | slice | bytes 12582912 | tf_op jit(solution)/shard_map/slice | solution.py:85
  143.0 19.0 %slice.98 = f32[34,49152]{0,1:T(8,128)} slice(f32[36,49152]{0,1:T(8,128)} %scatter_custom_fusion), slice={[1:35], [0:49152]} | slice | bytes 13369344 | tf_op jit(solution)/shard_map/slice | solution.py:84
  162.0 17.2 %copy.99 = f32[32,128,384]{2,1,0:T(8,128)} copy(f32[32,128,384]{0,2,1:T(8,128)} %bitcast.103) | data formatting | bytes 12582912 | tf_op jit(solution)/shard_map/slice | solution.py:85
  179.2 17.7 %copy.100 = f32[34,128,384]{2,1,0:T(8,128)} copy(f32[34,128,384]{0,2,1:T(8,128)} %bitcast.102) | data formatting | bytes 13369344 | tf_op jit(solution)/shard_map/slice | solution.py:84
  196.9 52.0 %all-reduce.3.cloned.1.call-done = f32[128,128]{1,0:T(8,128)} async-done(((f32[128,128]{1,0:T(8,128)}), f32[128,128]{1,0:T(8,128)}) %all-reduce.3.cloned.1.call-update) | async-done | bytes 65552 | tf_op jit(solution)/shard_map/psum | solution.py:59
  249.0 1.1 fusion.78
  250.1 1.1 fusion.76
  251.4 11.7 %cholesky.74 = f32[128,128]{1,0:T(8,128)S(1)} custom-call(f32[128,128]{1,0:T(8,128)S(1)} %fusion.63), custom_call_target="Cholesky" | custom-call | tf_op jit(solution)/shard_map/jit(cholesky)/cholesky | solution.py:52
  263.2 0.6 compare_reduce_fusion.3
  263.8 0.7 fusion.45
  264.5 9.8 %custom-call.10 = f32[1,128,128]{1,2,0:T(8,128)S(1)} custom-call(f32[1,128,128]{2,1,0:T(8,128)S(1)} %fusion.45), custom_call_target="InvertDiagBlocksLowerTriangular" | custom-call | tf_op jit(solution)/shard_map/jit(_solve_triangular)/triangular_solve | solution.py:53
  274.3 1.1 fusion.60
  275.4 1.1 fusion.73
  276.6 1.0 fusion.71
  278.1 11.7 %cholesky.85 = f32[128,128]{1,0:T(8,128)S(1)} custom-call(f32[128,128]{1,0:T(8,128)S(1)} %fusion.58), custom_call_target="Cholesky" | custom-call | tf_op jit(solution)/shard_map/jit(cholesky)/cholesky | solution.py:52
  289.9 0.6 compare_reduce_fusion.2
  290.5 0.7 fusion.46
  291.2 10.2 %custom-call.11 = f32[1,128,128]{1,2,0:T(8,128)S(1)} custom-call(f32[1,128,128]{2,1,0:T(8,128)S(1)} %fusion.46), custom_call_target="InvertDiagBlocksLowerTriangular" | custom-call | tf_op jit(solution)/shard_map/jit(_solve_triangular)/triangular_solve | solution.py:53
  301.7 3.5 fusion.22
  305.2 2.0 copy.87
  307.2 3.2 slice.96
  310.4 2.9 fusion.99
  313.3 3.1 copy.108
  316.5 1.9 copy.107
  318.4 3.2 copy.106
  321.5 11.8 %fusion.30 = f32[128,34,128]{0,2,1:T(8,128)S(1)} fusion(f32[34,128,384]{2,1,0:T(8,128)} %copy.100, f32[128,34,128]{2,0,1:T(8,128)} %copy.108, f32[128,34,128]{2,0,1:T(8,128)} %copy.107, f32[128,34,128]{2,0,1:T(8,128)} %copy.106), kind=kOutput, calls=%fused_computation.33 | convolution fusion | flops 2570256384 | bytes 15597568 | tf_op jit(solution)/shard_map/cbj,brj->cbr/dot_general | solution.py:39
  333.3 0.8 fusion.100
  334.1 7.7 %fusion.8 = f32[32,128,128]{2,1,0:T(8,128)} fusion(f32[32,128,384]{2,1,0:T(8,128)S(1)} %bitcast.106, f32[128,32,128]{0,2,1:T(8,128)S(1)} %get-tuple-element.12, f32[128,32,128]{0,2,1:T(8,128)S(1)} %get-tuple-element.13, f32[128,32,128]{0,2,1:T(8,128)S(1)} %get-tuple-element.11), kind=kOutput, calls=%fused_computation.9 | convolution fusion | flops 2419064832 | bytes 14680064 | tf_op jit(solution)/shard_map/cbj,brj->cbr/dot_general | solution.py:39
  341.9 3.2 copy.101
  345.1 6.5 %fusion.21 = f32[256,256]{1,0:T(8,128)} fusion(f32[128,4096]{1,0:T(8,128)} %copy.101, f32[128,4096]{1,0:T(8,128)S(1)} %copy-done.1), kind=kOutput, calls=%fused_computation.23 | convolution fusion | flops 3222274048 | bytes 4456448 | tf_op jit(solution)/shard_map/dot_general | solution.py:58
  351.6 128.0 %all-reduce.5.cloned.1.call-done = f32[256,256]{1,0:T(8,128)} async-done(((f32[256,256]{1,0:T(8,128)}), f32[256,256]{1,0:T(8,128)}) %all-reduce.5.cloned.1.call-update) | async-done | bytes 262160 | tf_op jit(solution)/shard_map/psum | solution.py:59
  479.6 1.0 broadcast_multiply_fusion
  481.0 0.4 fusion.41
  481.6 11.7 %cholesky.96 = f32[128,128]{1,0:T(8,128)S(1)} custom-call(f32[128,128]{1,0:T(8,128)S(1)} %fusion.53), custom_call_target="Cholesky" | custom-call | tf_op jit(solution)/shard_map/jit(cholesky)/cholesky | solution.py:52
  493.4 0.6 compare_reduce_fusion.1
  494.0 0.7 fusion.47
  494.7 9.8 %custom-call.12 = f32[1,128,128]{1,2,0:T(8,128)S(1)} custom-call(f32[1,128,128]{2,1,0:T(8,128)S(1)} %fusion.47), custom_call_target="InvertDiagBlocksLowerTriangular" | custom-call | tf_op jit(solution)/shard_map/jit(_solve_triangular)/triangular_solve | solution.py:53
  505.6 0.4 fusion.105
  506.2 11.9 %cholesky.107 = f32[128,128]{1,0:T(8,128)S(1)} custom-call(f32[128,128]{1,0:T(8,128)S(1)} %fusion.50), custom_call_target="Cholesky" | custom-call | tf_op jit(solution)/shard_map/jit(cholesky)/cholesky | solution.py:52
  518.1 0.6 compare_reduce_fusion
  518.8 0.7 fusion.48
  519.5 9.8 %custom-call.13 = f32[1,128,128]{1,2,0:T(8,128)S(1)} custom-call(f32[1,128,128]{2,1,0:T(8,128)S(1)} %fusion.48), custom_call_target="InvertDiagBlocksLowerTriangular" | custom-call | tf_op jit(solution)/shard_map/jit(_solve_triangular)/triangular_solve | solution.py:53
  529.6 5.2 fusion.20
  (65 shorter events, 4.0 us)
Async XLA Ops:
  6.5 13.0 %copy-start.7 = (s32[2]{0:T(128)S(1)}, s32[2]{0:T(128)}, u32[]{:S(2)}) copy-start(s32[2]{0:T(128)} %constant.56) | copy-start | bytes 28
  6.5 13.2 %copy-start.8 = (s32[2]{0:T(128)S(1)}, s32[2]{0:T(128)}, u32[]{:S(2)}) copy-start(s32[2]{0:T(128)} %constant.53) | copy-start | bytes 28
  6.5 7.7 %copy-start.5 = (f32[64,4096]{1,0:T(8,128)S(1)}, f32[64,4096]{1,0:T(8,128)}, u32[]{:S(2)}) copy-start(f32[64,4096]{1,0:T(8,128)} %param.8) | copy-start | bytes 3145732
  6.5 12.9 %copy-start.6 = (s32[128]{0:T(128)S(1)}, s32[128]{0:T(128)}, u32[]{:S(2)}) copy-start(s32[128]{0:T(128)} %param.10) | copy-start | bytes 1540
  6.5 242.4 %all-reduce.3.cloned.1.call-start = ((), (), s32[]{:S(2)}) async-start(), calls=%async_computation | async-start | bytes 131072 | tf_op jit(solution)/shard_map/psum | solution.py:59
  9.3 20.3 %collective-permute-start.3 = (f32[128,256]{0,1:T(8,128)}, f32[128,256]{0,1:T(8,128)S(1)}, u32[]{:S(2)}, u32[]{:S(2)}) collective-permute-start(f32[128,256]{0,1:T(8,128)} %get-tuple-element.15), channel_id=1, source_target_pairs={{1,0},{2,1},{3,2},{4,3},{5,4},{6,5},{7,6},{8,7},{9,8},{10,9},{11,1... | collective-permute-start | bytes 393224 | tf_op jit(solution)/shard_map/ppermute | solution.py:18
  10.6 19.0 %collective-permute-start.2 = (f32[128,256]{0,1:T(8,128)}, f32[128,256]{0,1:T(8,128)}, u32[]{:S(2)}, u32[]{:S(2)}) collective-permute-start(f32[128,256]{0,1:T(8,128)} %get-tuple-element.14), channel_id=1, source_target_pairs={{0,1},{1,2},{2,3},{3,4},{4,5},{5,6},{6,7},{7,8},{8,9},{9,10},{10,1... | collective-permute-start | bytes 393224 | tf_op jit(solution)/shard_map/ppermute | solution.py:15
  14.3 6.1 %collective-permute-start = (f32[64,384]{1,0:T(8,128)S(1)}, f32[64,384]{1,0:T(8,128)S(1)}, u32[]{:S(2)}, u32[]{:S(2)}) collective-permute-start(f32[64,384]{1,0:T(8,128)S(1)} %get-tuple-element.20), channel_id=1, source_target_pairs={{0,1},{1,2},{2,3},{3,4},{4,5},{5,6},{6,7},{7,8},{8,9},{9,10},{10,1... | collective-permute-start | bytes 294920 | tf_op jit(solution)/shard_map/ppermute | solution.py:15
  18.2 3.9 collective-permute-start.1
  91.7 17.8 %copy-start.2 = (f32[64,36,128]{2,0,1:T(8,128)S(1)}, f32[64,36,128]{2,0,1:T(8,128)}, u32[]{:S(2)}) copy-start(f32[64,36,128]{2,0,1:T(8,128)} %copy.105) | copy-start | bytes 3538948
  91.7 17.8 %copy-start.3 = (f32[64,36,128]{2,0,1:T(8,128)S(1)}, f32[64,36,128]{2,0,1:T(8,128)}, u32[]{:S(2)}) copy-start(f32[64,36,128]{2,0,1:T(8,128)} %copy.104) | copy-start | bytes 3538948
  124.0 355.6 %all-reduce.5.cloned.1.call-start = ((), (), s32[]{:S(2)}) async-start(), calls=%async_computation.1 | async-start | bytes 524288 | tf_op jit(solution)/shard_map/psum | solution.py:59
  313.3 3.1 copy-start
  318.4 15.7 %slice-start = ((s8[6291456]{0:T(1024)(128)(4,1)}), s8[2097152]{0:T(1024)(128)(4,1)S(1)}, s32[]{:S(2)}) async-start(s8[6291456]{0:T(1024)(128)(4,1)} %bitcast.105), calls=%async_computation.2 | async-start | bytes 4194304
  321.5 12.6 %slice-start.1 = ((s8[6291456]{0:T(1024)(128)(4,1)}), s8[4194304]{0:T(1024)(128)(4,1)S(1)}, s32[]{:S(2)}) async-start(s8[6291456]{0:T(1024)(128)(4,1)} %bitcast.105), calls=%async_computation.3 | async-start | bytes 8388608
  341.9 3.2 copy-start.1
  479.6 25.2 %copy-start.4 = (f32[256,256]{1,0:T(8,128)S(1)}, f32[256,256]{1,0:T(8,128)}, u32[]{:S(2)}) copy-start(f32[256,256]{1,0:T(8,128)} %all-reduce.5.cloned.1.call-done) | copy-start | bytes 786436
Sparse Core Ops, SparseCore 0:
  124.1 124.8 all-reduce.2
  351.7 127.8 all-reduce.4
where the time goes:
time: 549 us; the launch traced here: 542 us
  local copies, waits for them, and re-layouts  183 us (33%)
  waiting for transfers between devices  180 us (33%)
  other arithmetic  96.5 us (18%)
  matrix products  57.7 us (11%)
  between operations  14.2 us (3%)
  starting transfers between devices  10.2 us (2%)
    psum x2, waiting for transfers between devices, gram_total(): summed = lax.psum(local, 'rows')  180 us
    unnamed x32, local copies, waits for them, and re-layouts  66.7 us
    another operation x12, other arithmetic, compress(): factor = jnp.linalg.cholesky(metric)  49.7 us
    another operation x8, other arithmetic, compress(): coeffs = jax.scipy.linalg.solve_triangular(factor, spanning.T, lower=True)  42.2 us
    slice x2, local copies, waits for them, and re-layouts, body(): once_more = apply_band(factor_deep, blocked[1:-1])  36.8 us
    slice x2, local copies, waits for them, and re-layouts, body(): squared = apply_band(once_more, blocked[2:-2])  36.1 us
    dot_general x3, matrix products, apply_band(): jnp.einsum('cbj,brj->cbr', windows, blocked, precision=lax.Precision.HIGH...  31.5 us
    scatter x1, local copies, waits for them, and re-layouts, band_blocks(): return blocked.at[:, row_index, columns].set(values)  17.8 us
  transfers between devices with their start and end apart: 6, of which 2 were waited for; matrix products, arithmetic and copies ran while one was open for 15% of the time, Pallas kernels for 0%

commit v1 on v0

--- a/solution.py
+++ b/solution.py
@@ -56,7 +56,7 @@
 
 def gram_total(stacked, total):
     local = jnp.dot(stacked, stacked.T, precision=lax.Precision.HIGHEST)
-    summed = lax.psum(local, "rows")
+    summed = jnp.sum(lax.all_gather(local, "rows"), 0)
     return summed / total
 
 

time: 549 us -> 452 us (0.82)
  waiting for transfers between devices: 180 us -> 82.8 us
    psum x2 -> x0, waiting for transfers between devices: 180 us -> none  [gram_total(): summed = lax.psum(local, 'rows')]
    all_gather x0 -> x2, waiting for transfers between devices: none -> 82.8 us  [gram_total(): summed = jnp.sum(lax.all_gather(local, 'rows'), 0)]
    reduce_sum x0 -> x2, other arithmetic: none -> 5.63 us  [gram_total(): summed = jnp.sum(lax.all_gather(local, 'rows'), 0)]
    unnamed x32 -> x30, local copies, waits for them, and re-layouts: 66.7 us -> 66.7 us
  transfers between devices with their start and end apart: 6 -> 6, of which waited for: 2 -> 1; matrix products, arithmetic and copies ran while one was open for 15% -> 19% of each run, Pallas kernels for 0% -> 0%
where the time goes in v1:
time: 452 us; the launch traced here: 445 us
  local copies, waits for them, and re-layouts  183 us (40%)
  other arithmetic  101 us (22%)
  waiting for transfers between devices  82.8 us (18%)
  matrix products  53.7 us (12%)
  between operations  14.2 us (3%)
  starting transfers between devices  10.2 us (2%)
    all_gather x2, waiting for transfers between devices, gram_total(): summed = jnp.sum(lax.all_gather(local, 'rows'), 0)  82.8 us
    unnamed x30, local copies, waits for them, and re-layouts  66.7 us
    another operation x12, other arithmetic, compress(): factor = jnp.linalg.cholesky(metric)  49.6 us
    another operation x8, other arithmetic, compress(): coeffs = jax.scipy.linalg.solve_triangular(factor, spanning.T, lower=True)  42.2 us
    slice x2, local copies, waits for them, and re-layouts, body(): once_more = apply_band(factor_deep, blocked[1:-1])  36.6 us
    slice x2, local copies, waits for them, and re-layouts, body(): squared = apply_band(once_more, blocked[2:-2])  36.3 us
    dot_general x3, matrix products, apply_band(): jnp.einsum('cbj,brj->cbr', windows, blocked, precision=lax.Precision.HIGH...  31.5 us
    scatter x1, local copies, waits for them, and re-layouts, band_blocks(): return blocked.at[:, row_index, columns].set(values)  17.8 us
  transfers between devices with their start and end apart: 6, of which 1 were waited for; matrix products, arithmetic and copies ran while one was open for 19% of the time, Pallas kernels for 0%

profile of v1, /device:TPU:0, one launch (start us, length us, event | category | flops | bytes accessed | tf_op | source)
XLA Modules:
  0.0 445.0 jit_solution(2475284802687087528)
XLA Ops:
  6.6 2.0 copy.71
  8.6 0.7 fusion.101
  9.3 1.3 collective-permute-start.3
  10.6 3.7 collective-permute-start.2
  14.3 3.9 collective-permute-start
  18.2 1.3 collective-permute-start.1
  19.8 0.6 select_bitcast_fusion
  20.4 0.6 constant_dynamic-update-slice_fusion.2
  21.1 1.0 constant_dynamic-update-slice_fusion.1
  22.1 0.6 constant_dynamic-update-slice_fusion
  22.8 1.5 reshape.80
  24.5 1.4 slice.90
  25.9 1.2 copy.105
  27.1 1.2 copy.104
  28.3 1.2 copy.103
  29.6 2.5 pad_maximum_fusion.3
  32.0 8.6 %copy.98 = f32[128,128,36]{2,1,0:T(8,128)} copy(f32[128,128,36]{0,1,2:T(8,128)} %bitcast.111) | data formatting | bytes 4718592 | tf_op jit(solution)/shard_map/transpose | solution.py:26
  40.6 51.0 %scatter_custom_fusion = f32[36,49152]{0,1:T(8,128)} fusion(s32[16384]{0:T(1024)} %select_bitcast_fusion, f32[16384,36]{1,0:T(8,128)} %bitcast.114, f32[]{:T(128)} %constant.48.clone.1), kind=kCustom, calls=%fused_computation.1 | custom fusion | bytes 7078400
  91.7 17.8 %copy.79 = f32[36,128,384]{2,1,0:T(8,128)} copy(f32[36,128,384]{0,2,1:T(8,128)} %bitcast.103) | data formatting | bytes 14155776 | tf_op jit(solution)/shard_map/scatter | solution.py:31
  109.5 12.0 %fusion.33 = f32[36,8,8,128]{3,2,1,0:T(8,128)S(1)} fusion(f32[36,128,384]{2,1,0:T(8,128)} %copy.79, f32[64,36,128]{2,0,1:T(8,128)S(1)} %copy-done.2, f32[64,36,128]{2,0,1:T(8,128)S(1)} %copy-done.3, f32[64,36,128]{2,0,1:T(8,128)} %copy.103), kind=kOutput, calls=%fused_computation.34 | convolution fusion | flops 1360723968 | bytes 11796480 | tf_op jit(solution)/shard_map/cbj,brj->cbr/dot_general | solution.py:39
  121.5 2.4 fusion.26
  124.0 19.0 %slice.97 = f32[32,49152]{0,1:T(8,128)} slice(f32[36,49152]{0,1:T(8,128)} %scatter_custom_fusion), slice={[2:34], [0:49152]} | slice | bytes 12582912 | tf_op jit(solution)/shard_map/slice | solution.py:85
  143.0 19.0 %slice.98 = f32[34,49152]{0,1:T(8,128)} slice(f32[36,49152]{0,1:T(8,128)} %scatter_custom_fusion), slice={[1:35], [0:49152]} | slice | bytes 13369344 | tf_op jit(solution)/shard_map/slice | solution.py:84
  162.0 17.3 %copy.99 = f32[32,128,384]{2,1,0:T(8,128)} copy(f32[32,128,384]{0,2,1:T(8,128)} %bitcast.105) | data formatting | bytes 12582912 | tf_op jit(solution)/shard_map/slice | solution.py:85
  179.3 17.6 %copy.100 = f32[34,128,384]{2,1,0:T(8,128)} copy(f32[34,128,384]{0,2,1:T(8,128)} %bitcast.104) | data formatting | bytes 13369344 | tf_op jit(solution)/shard_map/slice | solution.py:84
  196.9 1.7 reduce_sum.18
  199.4 11.7 %cholesky.74 = f32[128,128]{1,0:T(8,128)S(1)} custom-call(f32[128,128]{1,0:T(8,128)S(1)} %fusion.63), custom_call_target="Cholesky" | custom-call | tf_op jit(solution)/shard_map/jit(cholesky)/cholesky | solution.py:52
  211.1 0.6 compare_reduce_fusion.3
  211.8 0.7 fusion.45
  212.4 9.8 %custom-call.10 = f32[1,128,128]{1,2,0:T(8,128)S(1)} custom-call(f32[1,128,128]{2,1,0:T(8,128)S(1)} %fusion.45), custom_call_target="InvertDiagBlocksLowerTriangular" | custom-call | tf_op jit(solution)/shard_map/jit(_solve_triangular)/triangular_solve | solution.py:53
  223.5 11.7 %cholesky.85 = f32[128,128]{1,0:T(8,128)S(1)} custom-call(f32[128,128]{1,0:T(8,128)S(1)} %fusion.58), custom_call_target="Cholesky" | custom-call | tf_op jit(solution)/shard_map/jit(cholesky)/cholesky | solution.py:52
  235.3 0.6 compare_reduce_fusion.2
  235.9 0.7 fusion.46
  236.6 10.2 %custom-call.11 = f32[1,128,128]{1,2,0:T(8,128)S(1)} custom-call(f32[1,128,128]{2,1,0:T(8,128)S(1)} %fusion.46), custom_call_target="InvertDiagBlocksLowerTriangular" | custom-call | tf_op jit(solution)/shard_map/jit(_solve_triangular)/triangular_solve | solution.py:53
  247.1 3.5 fusion.22
  250.6 2.0 copy.87
  252.6 3.2 slice.96
  255.8 2.9 fusion.99
  258.7 3.1 copy.108
  261.9 1.9 copy.107
  263.8 3.2 copy.106
  267.0 11.8 %fusion.30 = f32[128,34,128]{0,2,1:T(8,128)S(1)} fusion(f32[34,128,384]{2,1,0:T(8,128)} %copy.100, f32[128,34,128]{2,0,1:T(8,128)} %copy.108, f32[128,34,128]{2,0,1:T(8,128)} %copy.107, f32[128,34,128]{2,0,1:T(8,128)} %copy.106), kind=kOutput, calls=%fused_computation.33 | convolution fusion | flops 2570256384 | bytes 15597568 | tf_op jit(solution)/shard_map/cbj,brj->cbr/dot_general | solution.py:39
  278.7 0.8 fusion.100
  279.5 7.7 %fusion.8 = f32[32,128,128]{2,1,0:T(8,128)} fusion(f32[32,128,384]{2,1,0:T(8,128)S(1)} %bitcast.108, f32[128,32,128]{0,2,1:T(8,128)S(1)} %get-tuple-element.12, f32[128,32,128]{0,2,1:T(8,128)S(1)} %get-tuple-element.13, f32[128,32,128]{0,2,1:T(8,128)S(1)} %get-tuple-element.11), kind=kOutput, calls=%fused_computation.9 | convolution fusion | flops 2419064832 | bytes 14680064 | tf_op jit(solution)/shard_map/cbj,brj->cbr/dot_general | solution.py:39
  287.3 3.3 copy.101
  290.5 6.5 %fusion.21 = f32[256,256]{1,0:T(8,128)} fusion(f32[128,4096]{1,0:T(8,128)} %copy.101, f32[128,4096]{1,0:T(8,128)S(1)} %copy-done.1), kind=kOutput, calls=%fused_computation.23 | convolution fusion | flops 3222274048 | bytes 4456448 | tf_op jit(solution)/shard_map/dot_general | solution.py:58
  297.1 82.8 %all-gather.7.cloned.1.call-done = f32[8192,256]{1,0:T(8,128)} async-done(((f32[256,256]{1,0:T(8,128)}), f32[8192,256]{1,0:T(8,128)}) %all-gather.7.cloned.1.call-update) | async-done | bytes 8388624 | tf_op jit(solution)/shard_map/all_gather | solution.py:59
  379.8 3.9 reduce_sum.19
  383.8 0.4 fusion.43
  384.2 0.4 fusion.41
  384.8 11.7 %cholesky.96 = f32[128,128]{1,0:T(8,128)S(1)} custom-call(f32[128,128]{1,0:T(8,128)S(1)} %fusion.53), custom_call_target="Cholesky" | custom-call | tf_op jit(solution)/shard_map/jit(cholesky)/cholesky | solution.py:52
  396.5 0.6 compare_reduce_fusion.1
  397.2 0.7 fusion.47
  397.8 9.8 %custom-call.12 = f32[1,128,128]{1,2,0:T(8,128)S(1)} custom-call(f32[1,128,128]{2,1,0:T(8,128)S(1)} %fusion.47), custom_call_target="InvertDiagBlocksLowerTriangular" | custom-call | tf_op jit(solution)/shard_map/jit(_solve_triangular)/triangular_solve | solution.py:53
  407.7 0.3 fusion.38
  408.0 0.4 fusion.98
  408.4 0.6 fusion.97
  409.0 0.4 fusion.105
  409.6 11.7 %cholesky.107 = f32[128,128]{1,0:T(8,128)S(1)} custom-call(f32[128,128]{1,0:T(8,128)S(1)} %fusion.50), custom_call_target="Cholesky" | custom-call | tf_op jit(solution)/shard_map/jit(cholesky)/cholesky | solution.py:52
  421.3 0.6 compare_reduce_fusion
  422.0 0.7 fusion.48
  422.6 9.8 %custom-call.13 = f32[1,128,128]{1,2,0:T(8,128)S(1)} custom-call(f32[1,128,128]{2,1,0:T(8,128)S(1)} %fusion.48), custom_call_target="InvertDiagBlocksLowerTriangular" | custom-call | tf_op jit(solution)/shard_map/jit(_solve_triangular)/triangular_solve | solution.py:53
  432.4 0.3 fusion.36
  432.8 5.2 %fusion.20 = f32[128,4096]{1,0:T(8,128)} fusion(f32[128,256]{1,0:T(8,128)S(1)} %fusion.36, f32[128,4096]{1,0:T(8,128)} %copy.101, f32[128,4096]{1,0:T(8,128)S(1)} %copy-done.1), kind=kOutput, calls=%fused_computation.22 | convolution fusion | flops 1611661312 | bytes 6422528 | tf_op jit(solution)/shard_map/dot_general | solution.py:88
  (65 shorter events, 3.6 us)
Async XLA Ops:
  6.5 13.0 %copy-start.6 = (s32[2]{0:T(128)S(1)}, s32[2]{0:T(128)}, u32[]{:S(2)}) copy-start(s32[2]{0:T(128)} %constant.57) | copy-start | bytes 28
  6.5 13.2 %copy-start.7 = (s32[2]{0:T(128)S(1)}, s32[2]{0:T(128)}, u32[]{:S(2)}) copy-start(s32[2]{0:T(128)} %constant.54) | copy-start | bytes 28
  6.5 7.7 %copy-start.4 = (f32[64,4096]{1,0:T(8,128)S(1)}, f32[64,4096]{1,0:T(8,128)}, u32[]{:S(2)}) copy-start(f32[64,4096]{1,0:T(8,128)} %param.8) | copy-start | bytes 3145732
  6.5 12.9 %copy-start.5 = (s32[128]{0:T(128)S(1)}, s32[128]{0:T(128)}, u32[]{:S(2)}) copy-start(s32[128]{0:T(128)} %param.10) | copy-start | bytes 1540
  6.5 190.4 %all-gather.5.cloned.1.call-start = ((), (), s32[]{:S(2)}) async-start(), calls=%async_computation | async-start | bytes 2162688 | tf_op jit(solution)/shard_map/all_gather | solution.py:59
  9.3 20.3 %collective-permute-start.3 = (f32[128,256]{0,1:T(8,128)}, f32[128,256]{0,1:T(8,128)S(1)}, u32[]{:S(2)}, u32[]{:S(2)}) collective-permute-start(f32[128,256]{0,1:T(8,128)} %get-tuple-element.15), channel_id=1, source_target_pairs={{1,0},{2,1},{3,2},{4,3},{5,4},{6,5},{7,6},{8,7},{9,8},{10,9},{11,1... | collective-permute-start | bytes 393224 | tf_op jit(solution)/shard_map/ppermute | solution.py:18
  10.6 19.0 %collective-permute-start.2 = (f32[128,256]{0,1:T(8,128)}, f32[128,256]{0,1:T(8,128)}, u32[]{:S(2)}, u32[]{:S(2)}) collective-permute-start(f32[128,256]{0,1:T(8,128)} %get-tuple-element.14), channel_id=1, source_target_pairs={{0,1},{1,2},{2,3},{3,4},{4,5},{5,6},{6,7},{7,8},{8,9},{9,10},{10,1... | collective-permute-start | bytes 393224 | tf_op jit(solution)/shard_map/ppermute | solution.py:15
  14.3 6.1 %collective-permute-start = (f32[64,384]{1,0:T(8,128)S(1)}, f32[64,384]{1,0:T(8,128)S(1)}, u32[]{:S(2)}, u32[]{:S(2)}) collective-permute-start(f32[64,384]{1,0:T(8,128)S(1)} %get-tuple-element.20), channel_id=1, source_target_pairs={{0,1},{1,2},{2,3},{3,4},{4,5},{5,6},{6,7},{7,8},{8,9},{9,10},{10,1... | collective-permute-start | bytes 294920 | tf_op jit(solution)/shard_map/ppermute | solution.py:15
  18.2 3.9 collective-permute-start.1
  91.7 17.8 %copy-start.2 = (f32[64,36,128]{2,0,1:T(8,128)S(1)}, f32[64,36,128]{2,0,1:T(8,128)}, u32[]{:S(2)}) copy-start(f32[64,36,128]{2,0,1:T(8,128)} %copy.105) | copy-start | bytes 3538948
  91.7 17.8 %copy-start.3 = (f32[64,36,128]{2,0,1:T(8,128)S(1)}, f32[64,36,128]{2,0,1:T(8,128)}, u32[]{:S(2)}) copy-start(f32[64,36,128]{2,0,1:T(8,128)} %copy.104) | copy-start | bytes 3538948
  124.0 255.8 %all-gather.7.cloned.1.call-start = ((), (), s32[]{:S(2)}) async-start(), calls=%async_computation.1 | async-start | bytes 8650752 | tf_op jit(solution)/shard_map/all_gather | solution.py:59
  258.7 3.1 copy-start
  263.8 15.7 %slice-start = ((s8[6291456]{0:T(1024)(128)(4,1)}), s8[2097152]{0:T(1024)(128)(4,1)S(1)}, s32[]{:S(2)}) async-start(s8[6291456]{0:T(1024)(128)(4,1)} %bitcast.107), calls=%async_computation.2 | async-start | bytes 4194304
  267.0 12.6 %slice-start.1 = ((s8[6291456]{0:T(1024)(128)(4,1)}), s8[4194304]{0:T(1024)(128)(4,1)S(1)}, s32[]{:S(2)}) async-start(s8[6291456]{0:T(1024)(128)(4,1)} %bitcast.107), calls=%async_computation.3 | async-start | bytes 8388608
  287.3 3.3 copy-start.1
Sparse Core Ops, SparseCore 0:
  124.1 61.6 all-gather.4
  297.2 82.5 all-gather.6
